TPU v7x, 128 devices: a whole 4x4x4 slice. The times are simulated.
128 devices in a mesh: patch: 64 (over y, x_hi, z, core), band: 2 (over x_lo).
Axes of the slice: x: 4 (x_hi: 2, x_lo: 2; x = x_hi * 2 + x_lo), y: 4, z: 4, core: 2. Of those that a mesh axis runs over, the one named last changes fastest.
Arguments:
- latents: float32 [40960, 512], P('patch', 'band'), may hold values from -6 to 6
- edge_latents: float32 [327680, 512], P(('patch', 'band')), may hold values from -6 to 6
- edge_sender: int32 [327680], P(('patch', 'band')), may hold values from 0 to 1343, as said below
- edge_receiver: int32 [327680], P(('patch', 'band')), may hold values from 0 to 319
- block_counts: int32 [2560], P(('patch', 'band')), may hold values from 16 to 128, as said below
- send_rows: int32 [128, 128, 8], P(('patch', 'band')), may hold values from 0 to 319
- edge_first_weight: bfloat16 [2, 1536, 512], replicated, may hold values from -0.15625 to 0.15625
- edge_first_bias: float32 [2, 512], replicated, may hold values from -3 to 3
- edge_second_weight: bfloat16 [2, 512, 512], replicated
- edge_gain: float32 [2, 512], replicated, may hold values from 0.1 to 1.9
- edge_offset: float32 [2, 512], replicated, may hold values from -3 to 3
- node_first_weight: bfloat16 [2, 1024, 512], replicated, may hold values from -0.1875 to 0.1875
- node_first_bias: float32 [2, 512], replicated, may hold values from -3 to 3
- node_second_weight: bfloat16 [2, 512, 512], replicated
- node_gain: float32 [2, 512], replicated, may hold values from 0.1 to 1.9
- node_offset: float32 [2, 512], replicated, may hold values from -3 to 3
Outputs:
- new_nodes: float32 [40960, 512], P(('patch', 'band'))
- new_edges: float32 [327680, 512], P(('patch', 'band'))
Inputs may be any that keep to these rules, and one draw needn't show every extreme that they name: `edge_sender`: an entry below 320 names a node row of the edge's own device; an entry k above names slot (k - 320) % 8 of the rows that device (k - 320) // 8 sends to the edge's device. `block_counts`: the used slots of a block are its first ones; every device has a full block. send_rows[d, q] lists node rows of device d, numbered within d, that device q receives from d.
All inputs are finite; a program needn't handle non-finite values.
Results may differ from a plain program's by a relative error of at most 0.0045.
Values may be sent and summed in bfloat16 or wider, within the bound.
A program may use at most 128 MiB of HBM per device.

v0:
```python
import jax
import jax.numpy as jnp
from jax import lax
from jax.sharding import PartitionSpec as P

epsilon = 1e-05


def layer_norm(values, norm_gain, norm_offset):
    centre = values - jnp.mean(values, axis=-1, keepdims=True)
    spread = jnp.mean(centre * centre, axis=-1, keepdims=True)
    return centre * lax.rsqrt(spread + epsilon) * norm_gain + norm_offset


def perceptron(pieces, first_weight, first_bias, second_weight, norm_gain, norm_offset):
    columns = pieces[0].shape[1]
    running = first_bias
    for position in range(len(pieces)):
        running = running + jnp.dot(
            pieces[position],
            first_weight[position * columns : (position + 1) * columns],
            preferred_element_type=jnp.float32,
        )
    active = (running * jax.nn.sigmoid(running)).astype(jnp.bfloat16)
    result = jnp.dot(active, second_weight, preferred_element_type=jnp.float32)
    return layer_norm(result, norm_gain, norm_offset)


def fetch_halo(node_low, send_lists):
    outgoing = node_low[send_lists]
    return lax.all_to_all(outgoing, ("patch", "band"), split_axis=0, concat_axis=0, tiled=True)


def shards(
    latents,
    edge_latents,
    edge_sender,
    edge_receiver,
    block_counts,
    send_rows,
    edge_first_weight,
    edge_first_bias,
    edge_second_weight,
    edge_gain,
    edge_offset,
    node_first_weight,
    node_first_bias,
    node_second_weight,
    node_gain,
    node_offset,
):
    layers = edge_first_weight.shape[0]
    send_lists = send_rows[0]
    block_length = edge_sender.shape[0] // block_counts.shape[0]
    usable = (jnp.arange(block_length, dtype=jnp.int32)[None, :] < block_counts[:, None]).reshape(
        -1
    )
    first_rows = None
    node_state = lax.all_to_all(latents, "band", split_axis=0, concat_axis=1, tiled=True)
    edge_state = edge_latents
    node_count = node_state.shape[0]
    matches = jnp.arange(node_count, dtype=jnp.int32)[:, None] == edge_receiver[None, :]
    receiver_hot = matches.astype(jnp.bfloat16)
    summing_hot = (matches & usable[None, :]).astype(jnp.bfloat16)
    for layer_index in range(layers):
        node_low = node_state.astype(jnp.bfloat16)
        incoming = fetch_halo(node_low, send_lists)
        sender_table = jnp.concatenate([node_low, incoming.reshape(-1, node_low.shape[1])], axis=0)
        receiver_rows = lax.dot_general(
            receiver_hot, node_low, (((0,), (0,)), ((), ())), preferred_element_type=jnp.float32
        ).astype(jnp.bfloat16)
        edge_low = edge_state.astype(jnp.bfloat16)
        update = perceptron(
            (edge_low, sender_table[edge_sender], receiver_rows),
            edge_first_weight[layer_index],
            edge_first_bias[layer_index],
            edge_second_weight[layer_index],
            edge_gain[layer_index],
            edge_offset[layer_index],
        )
        edge_state = edge_state + jnp.where(usable[:, None], update, jnp.zeros_like(update))
        edge_out_low = edge_state.astype(jnp.bfloat16)
        summed = jnp.dot(summing_hot, edge_out_low, preferred_element_type=jnp.float32)
        summed_low = summed.astype(jnp.bfloat16)
        node_state = node_state + perceptron(
            (node_low, summed_low),
            node_first_weight[layer_index],
            node_first_bias[layer_index],
            node_second_weight[layer_index],
            node_gain[layer_index],
            node_offset[layer_index],
        )
    return (node_state, edge_state)


def solution(mesh):
    return jax.shard_map(
        shards,
        mesh=mesh,
        in_specs=(
            P("patch", "band"),
            P(("patch", "band"), None),
            P(("patch", "band")),
            P(("patch", "band")),
            P(("patch", "band")),
            P(("patch", "band"), None, None),
            P(),
            P(),
            P(),
            P(),
            P(),
            P(),
            P(),
            P(),
            P(),
            P(),
        ),
        out_specs=(P(("patch", "band"), None), P(("patch", "band"), None)),
        check_vma=False,
    )
```

profile of v0, /device:TPU:1, one launch (start us, length us, event | category | flops | bytes accessed | tf_op | source)
XLA Modules:
  0.0 172.8 jit_solution(914075629936271546)
XLA Ops:
  0.6 3.5 %all-to-all-start = ((f32[2,320,256]{2,1,0:T(8,128)}), f32[2,320,256]{2,1,0:T(8,128)S(1)}, u32[]{:S(2)}, u32[]{:S(2)}) async-start(f32[2,320,256]{2,1,0:T(8,128)} %bitcast.107), calls=%async_computation | async-start | bytes 1310720 | tf_op jit(solution)/shard_map/all_to_all | solution.py:59
  4.2 0.7 compare_select_fusion.1
  4.9 0.1 copy.31
  5.0 0.1 reshape.133
  5.1 0.8 fusion.90
  5.8 0.8 fusion.88
  6.6 0.8 fusion.89
  7.4 0.8 fusion.91
  8.1 0.8 fusion.86
  8.9 6.4 %fusion.6 = f32[2560,512]{1,0:T(8,128)} fusion(f32[2560,512]{1,0:T(8,128)} %param.17, bf16[2,1536,512]{2,1,0:T(8,128)(2,1)} %param.22), kind=kOutput, calls=%fused_computation.17 | convolution fusion | flops 1343488000 | bytes 11010048 | tf_op jit(solution)/shard_map/dot_general | solution.py:19
  15.3 0.0 copy-done.9
  15.3 0.1 fusion.82
  15.4 0.0 copy-done.7
  15.4 0.0 all-to-all-done
  15.4 0.1 copy.34
  15.6 5.1 %gather_fusion = bf16[1024,512]{1,0:T(8,128)(2,1)} fusion(bf16[320,512]{1,0:T(8,128)(2,1)S(1)} %convert_element_type.50, s32[1024]{0:T(1024)S(1)} %broadcast_clamp_fusion), kind=kCustom, calls=%fused_computation | custom fusion | bytes 2101248 | tf_op jit(solution)/shard_map/gather | solution.py:30
  20.7 12.5 %all-to-all-start.1 = ((bf16[128,8,512]{2,1,0:T(8,128)(2,1)}), bf16[128,8,512]{2,1,0:T(8,128)(2,1)}, u32[]{:S(2)}, u32[]{:S(2)}) async-start(bf16[128,8,512]{2,1,0:T(8,128)(2,1)} %bitcast.104), calls=%async_computation.1 | async-start | bytes 2097152 | tf_op jit(solution)/shard_map/all_to_all | solution.py:31
  33.2 0.0 copy-start.8
  33.2 0.0 copy-start.12
  33.2 5.9 %copy.32 = f32[2560,512]{0,1:T(8,128)} copy(f32[2560,512]{1,0:T(8,128)} %param.17) | data formatting | bytes 10485760 | tf_op args[1]
  39.1 0.0 copy-done.8
  39.2 2.2 %convolution_add_fusion.3 = f32[320,512]{1,0:T(8,128)} fusion(bf16[320,512]{1,0:T(8,128)(2,1)S(1)} %bitcast.106, bf16[2,1024,512]{2,1,0:T(8,128)(2,1)} %param.27, f32[512]{0:T(512)S(1)} %bitcast.115), kind=kOutput, calls=%fused_computation.35 | convolution fusion | flops 167936000 | bytes 1509376 | tf_op jit(solution)/shard_map/dot_general | solution.py:19
  41.4 0.0 copy-done.12
  41.4 3.0 %convolution_convert_fusion.1 = bf16[2560,512]{1,0:T(8,128)(2,1)} fusion(bf16[320,512]{1,0:T(8,128)(2,1)S(1)} %convert_element_type.50, s32[2560]{0:T(1024)S(1)} %copy-done.12), kind=kOutput, calls=%fused_computation.11 | convolution fusion | flops 840990720 | bytes 2959360 | tf_op jit(solution)/shard_map/dot_general | solution.py:69
  44.4 8.1 %all-to-all-done.1 = bf16[128,8,512]{2,1,0:T(8,128)(2,1)} async-done(((bf16[128,8,512]{2,1,0:T(8,128)(2,1)}), bf16[128,8,512]{2,1,0:T(8,128)(2,1)}, u32[]{:S(2)}, u32[]{:S(2)}) %all-to-all-start.1) | async-done | bytes 1048608 | tf_op jit(solution)/shard_map/all_to_all | solution.py:31
  52.6 1.3 pad_maximum_fusion
  53.9 8.2 %gather_fusion.1 = bf16[2560,512]{1,0:T(8,128)(2,1)} fusion(bf16[1344,512]{1,0:T(8,128)(2,1)S(1)} %pad_maximum_fusion, s32[3072]{0:T(1024)S(1)} %pad_clamp_fusion), kind=kCustom, calls=%fused_computation.1 | custom fusion | bytes 5253120 | tf_op jit(solution)/shard_map/gather | solution.py:74
  62.1 5.8 %fusion.61 = f32[2560,512]{1,0:T(8,128)} fusion(bf16[2560,512]{1,0:T(8,128)(2,1)} %gather_fusion.1, bf16[2,1536,512]{2,1,0:T(8,128)(2,1)} %param.22), kind=kOutput, calls=%fused_computation.59 | convolution fusion | flops 1342177280 | bytes 8388608 | tf_op jit(solution)/shard_map/dot_general | solution.py:19
  67.9 0.0 copy-done.10
  67.9 11.1 %fusion.92 = (f32[2560]{0:T(1024)S(1)}, f32[2560,512]{0,1:T(8,128)}) fusion(bf16[2,512,512]{2,1,0:T(8,128)(2,1)S(1)} %copy-done.10, f32[2560,512]{1,0:T(8,128)} %fusion.61, f32[2560,512]{1,0:T(8,128)} %fusion.6, bf16[2560,512]{1,0:T(8,128)(2,1)} %convolution_convert_fusion.1, f32[512]{0:T(512)S(1)} %bitcast.121, bf16[2,1536,512]{2,1,0:T(8,128)(2,1)} %param.22), kind=kOutput, calls=%fused_computation.101 | convolution fusion | flops 2696148480 | bytes 19410944 | tf_op jit(solution)/shard_map/dot_general | solution.py:25
  79.0 3.2 %multiply_reduce_fusion.1 = f32[2560]{0:T(1024)S(1)} fusion(f32[2560,512]{0,1:T(8,128)} %get-tuple-element.23, f32[2560]{0:T(1024)S(1)} %broadcast_multiply_fusion.1), kind=kLoop, calls=%fused_computation.8 | loop fusion | flops 3929600 | bytes 5263360 | tf_op jit(solution)/shard_map/reduce_sum | solution.py:11
  82.2 0.8 copy-done.1
  83.0 6.3 %select_add_fusion.1 = f32[2560,512]{0,1:T(8,128)} fusion(f32[2560,512]{0,1:T(8,128)} %copy.32, f32[2560,512]{0,1:T(8,128)S(1)} %copy-done.1, f32[512]{0:T(512)S(1)} %bitcast.119, f32[512]{0:T(512)S(1)} %bitcast.118, f32[2560]{0:T(1024)S(1)} %add_rsqrt_fusion.1, f32[2560]{0:T(1024)S(1)} %broadcast_multiply_fusion.1, pred[2560]{0:T(1024)(128)(4,1)S(1)} %fusion.82), kind=kLoop, calls=%fused_computation.7 | loop fusion | flops 7864320 | bytes 15755776 | tf_op jit(solution)/shard_map/add | solution.py:81
  89.3 0.0 copy-done.6
  89.3 4.1 %multiply_convert_fusion.3 = bf16[320,512]{1,0:T(8,128)(2,1)S(1)} fusion(f32[320,512]{1,0:T(8,128)S(1)} %copy-done.6, f32[2560,512]{0,1:T(8,128)} %select_add_fusion.1, s32[2560]{0:T(1024)S(1)} %copy-done.12, pred[2560]{0:T(1024)(128)(4,1)S(1)} %fusion.82, bf16[2,1024,512]{2,1,0:T(8,128)(2,1)} %param.27), kind=kOutput, calls=%fused_computation.44 | convolution fusion | flops 1010728960 | bytes 6763008 | tf_op jit(solution)/shard_map/dot_general | solution.py:19
  93.4 0.0 copy-done.3
  93.4 0.4 fusion.95
  93.8 0.2 multiply_reduce_fusion.3
  94.1 0.2 fusion.85
  94.3 5.1 %gather_fusion.2 = bf16[1024,512]{1,0:T(8,128)(2,1)} fusion(bf16[320,512]{1,0:T(8,128)(2,1)S(1)} %fusion.85, s32[1024]{0:T(1024)S(1)} %broadcast_clamp_fusion), kind=kCustom, calls=%fused_computation.2 | custom fusion | bytes 2101248 | tf_op jit(solution)/shard_map/gather | solution.py:30
  99.4 4.1 %all-to-all-start.2 = ((bf16[128,8,512]{2,1,0:T(8,128)(2,1)}), bf16[128,8,512]{2,1,0:T(8,128)(2,1)S(1)}, u32[]{:S(2)}, u32[]{:S(2)}) async-start(bf16[128,8,512]{2,1,0:T(8,128)(2,1)} %bitcast.23), calls=%async_computation.2 | async-start | bytes 2097152 | tf_op jit(solution)/shard_map/all_to_all | solution.py:31
  103.5 0.0 slice-start
  103.5 2.4 %convolution_add_fusion.1 = f32[320,512]{1,0:T(8,128)} fusion(bf16[320,512]{1,0:T(8,128)(2,1)S(1)} %fusion.85, bf16[2,1024,512]{2,1,0:T(8,128)(2,1)} %param.27, f32[512]{0:T(512)S(1)} %bitcast.114), kind=kOutput, calls=%fused_computation.33 | convolution fusion | flops 167936000 | bytes 1509376 | tf_op jit(solution)/shard_map/dot_general | solution.py:19
  105.9 3.0 %convolution_convert_fusion = bf16[2560,512]{1,0:T(8,128)(2,1)} fusion(bf16[320,512]{1,0:T(8,128)(2,1)S(1)} %fusion.85, s32[2560]{0:T(1024)S(1)} %copy-done.12), kind=kOutput, calls=%fused_computation.10 | convolution fusion | flops 840990720 | bytes 2959360 | tf_op jit(solution)/shard_map/dot_general | solution.py:69
  108.9 0.0 slice-done
  108.9 0.0 slice-done.1
  108.9 4.9 %fusion.16 = f32[2560,512]{1,0:T(8,128)} fusion(f32[2560,512]{0,1:T(8,128)S(1)} %bitcast.99, bf16[2,1536,512]{2,1,0:T(8,128)(2,1)} %param.22), kind=kOutput, calls=%fused_computation.29 | convolution fusion | flops 1343488000 | bytes 11010048 | tf_op jit(solution)/shard_map/dot_general | solution.py:19
  113.9 9.5 %all-to-all-done.2 = bf16[128,8,512]{2,1,0:T(8,128)(2,1)S(1)} async-done(((bf16[128,8,512]{2,1,0:T(8,128)(2,1)}), bf16[128,8,512]{2,1,0:T(8,128)(2,1)S(1)}, u32[]{:S(2)}, u32[]{:S(2)}) %all-to-all-start.2) | async-done | bytes 1048608 | tf_op jit(solution)/shard_map/all_to_all | solution.py:31
  123.4 1.0 copy-done.2
  124.4 1.3 pad_maximum_fusion.1
  125.7 8.2 %gather_fusion.3 = bf16[2560,512]{1,0:T(8,128)(2,1)} fusion(bf16[1344,512]{1,0:T(8,128)(2,1)S(1)} %pad_maximum_fusion.1, s32[3072]{0:T(1024)S(1)} %pad_clamp_fusion), kind=kCustom, calls=%fused_computation.3 | custom fusion | bytes 5253120 | tf_op jit(solution)/shard_map/gather | solution.py:74
  133.9 5.8 %fusion.51 = f32[2560,512]{1,0:T(8,128)} fusion(bf16[2560,512]{1,0:T(8,128)(2,1)} %gather_fusion.3, bf16[2,1536,512]{2,1,0:T(8,128)(2,1)} %param.22), kind=kOutput, calls=%fused_computation.50 | convolution fusion | flops 1342177280 | bytes 8388608 | tf_op jit(solution)/shard_map/dot_general | solution.py:19
  139.7 0.0 copy-done.11
  139.7 11.1 %fusion.96 = (f32[2560]{0:T(1024)S(1)}, f32[2560,512]{0,1:T(8,128)}) fusion(bf16[2,512,512]{2,1,0:T(8,128)(2,1)S(1)} %copy-done.11, f32[2560,512]{1,0:T(8,128)} %fusion.51, f32[2560,512]{1,0:T(8,128)} %fusion.16, bf16[2560,512]{1,0:T(8,128)(2,1)} %convolution_convert_fusion, f32[512]{0:T(512)S(1)} %bitcast.120, bf16[2,1536,512]{2,1,0:T(8,128)(2,1)} %param.22), kind=kOutput, calls=%fused_computation.103 | convolution fusion | flops 2696148480 | bytes 19410944 | tf_op jit(solution)/shard_map/dot_general | solution.py:25
  150.8 3.2 %multiply_reduce_fusion = f32[2560]{0:T(1024)S(1)} fusion(f32[2560,512]{0,1:T(8,128)} %get-tuple-element.27, f32[2560]{0:T(1024)S(1)} %broadcast_multiply_fusion), kind=kLoop, calls=%fused_computation.5 | loop fusion | flops 3929600 | bytes 5263360 | tf_op jit(solution)/shard_map/reduce_sum | solution.py:11
  154.0 0.8 copy-done
  154.8 6.2 %select_add_fusion = f32[2560,512]{0,1:T(8,128)} fusion(f32[2560,512]{0,1:T(8,128)} %select_add_fusion.1, f32[2560,512]{0,1:T(8,128)S(1)} %copy-done, f32[512]{0:T(512)S(1)} %bitcast.117, f32[512]{0:T(512)S(1)} %bitcast.116, f32[2560]{0:T(1024)S(1)} %add_rsqrt_fusion, f32[2560]{0:T(1024)S(1)} %broadcast_multiply_fusion, pred[2560]{0:T(1024)(128)(4,1)S(1)} %fusion.82), kind=kLoop, calls=%fused_computation.4 | loop fusion | flops 7864320 | bytes 15755776 | tf_op jit(solution)/shard_map/add | solution.py:81
  161.0 5.9 %copy.33 = f32[2560,512]{1,0:T(8,128)} copy(f32[2560,512]{0,1:T(8,128)} %select_add_fusion) | data formatting | bytes 10485760
  166.9 0.0 copy-done.5
  166.9 4.1 %multiply_convert_fusion.2 = bf16[320,512]{1,0:T(8,128)(2,1)S(1)} fusion(f32[320,512]{1,0:T(8,128)S(1)} %copy-done.5, f32[2560,512]{0,1:T(8,128)} %select_add_fusion, s32[2560]{0:T(1024)S(1)} %copy-done.12, pred[2560]{0:T(1024)(128)(4,1)S(1)} %fusion.82, bf16[2,1024,512]{2,1,0:T(8,128)(2,1)} %param.27), kind=kOutput, calls=%fused_computation.41 | convolution fusion | flops 1010728960 | bytes 6763008 | tf_op jit(solution)/shard_map/dot_general | solution.py:19
  171.0 0.0 copy-done.4
  171.0 0.4 fusion.99
  171.4 0.2 multiply_reduce_fusion.2
  171.7 1.1 add_add_fusion
  (28 shorter events, 0.2 us)
Async XLA Ops:
  0.6 14.8 %all-to-all-start = ((f32[2,320,256]{2,1,0:T(8,128)}), f32[2,320,256]{2,1,0:T(8,128)S(1)}, u32[]{:S(2)}, u32[]{:S(2)}) async-start(f32[2,320,256]{2,1,0:T(8,128)} %bitcast.107), calls=%async_computation | async-start | bytes 1310720 | tf_op jit(solution)/shard_map/all_to_all | solution.py:59
  8.9 6.4 %copy-start.9 = (s32[20]{0:T(128)S(1)}, s32[20]{0:T(128)}, u32[]{:S(2)}) copy-start(s32[20]{0:T(128)} %param.20) | copy-start | bytes 244
  8.9 6.5 %copy-start.7 = (s32[2560]{0:T(1024)S(1)}, s32[2560]{0:T(1024)}, u32[]{:S(2)}) copy-start(s32[2560]{0:T(1024)} %param.18) | copy-start | bytes 30724
  20.7 31.9 %all-to-all-start.1 = ((bf16[128,8,512]{2,1,0:T(8,128)(2,1)}), bf16[128,8,512]{2,1,0:T(8,128)(2,1)}, u32[]{:S(2)}, u32[]{:S(2)}) async-start(bf16[128,8,512]{2,1,0:T(8,128)(2,1)} %bitcast.104), calls=%async_computation.1 | async-start | bytes 2097152 | tf_op jit(solution)/shard_map/all_to_all | solution.py:31
  33.2 5.9 %copy-start.8 = (f32[2,512]{1,0:T(2,128)S(1)}, f32[2,512]{1,0:T(2,128)}, u32[]{:S(2)}) copy-start(f32[2,512]{1,0:T(2,128)} %param.31) | copy-start | bytes 12292
  33.2 8.2 %copy-start.12 = (s32[2560]{0:T(1024)S(1)}, s32[2560]{0:T(1024)}, u32[]{:S(2)}) copy-start(s32[2560]{0:T(1024)} %param.19) | copy-start | bytes 30724
  62.1 5.8 %copy-start.10 = (bf16[2,512,512]{2,1,0:T(8,128)(2,1)S(1)}, bf16[2,512,512]{2,1,0:T(8,128)(2,1)}, u32[]{:S(2)}) copy-start(bf16[2,512,512]{2,1,0:T(8,128)(2,1)} %param.24) | copy-start | bytes 3145732
  78.9 4.0 %copy-start.1 = (f32[2560,512]{0,1:T(8,128)S(1)}, f32[2560,512]{0,1:T(8,128)}, u32[]{:S(2)}) copy-start(f32[2560,512]{0,1:T(8,128)} %get-tuple-element.23) | copy-start | bytes 15728644
  83.0 6.3 %copy-start.6 = (f32[320,512]{1,0:T(8,128)S(1)}, f32[320,512]{1,0:T(8,128)}, u32[]{:S(2)}) copy-start(f32[320,512]{1,0:T(8,128)} %convolution_add_fusion.3) | copy-start | bytes 1966084
  89.3 4.1 %copy-start.3 = (bf16[2,512,512]{2,1,0:T(8,128)(2,1)S(1)}, bf16[2,512,512]{2,1,0:T(8,128)(2,1)}, u32[]{:S(2)}) copy-start(bf16[2,512,512]{2,1,0:T(8,128)(2,1)} %param.29) | copy-start | bytes 3145732
  99.4 24.0 %all-to-all-start.2 = ((bf16[128,8,512]{2,1,0:T(8,128)(2,1)}), bf16[128,8,512]{2,1,0:T(8,128)(2,1)S(1)}, u32[]{:S(2)}, u32[]{:S(2)}) async-start(bf16[128,8,512]{2,1,0:T(8,128)(2,1)} %bitcast.23), calls=%async_computation.2 | async-start | bytes 2097152 | tf_op jit(solution)/shard_map/all_to_all | solution.py:31
  103.5 5.4 %slice-start = ((s8[5242880]{0:T(1024)(128)(4,1)}), s8[4194304]{0:T(1024)(128)(4,1)S(1)}, s32[]{:S(2)}) async-start(s8[5242880]{0:T(1024)(128)(4,1)} %bitcast.98), calls=%async_computation.3 | async-start | bytes 8388608
  105.9 3.1 %slice-start.1 = ((s8[5242880]{0:T(1024)(128)(4,1)}), s8[1048576]{0:T(1024)(128)(4,1)S(1)}, s32[]{:S(2)}) async-start(s8[5242880]{0:T(1024)(128)(4,1)} %bitcast.98), calls=%async_computation.4 | async-start | bytes 2097152
  123.4 1.0 copy-start.2
  133.9 5.8 %copy-start.11 = (bf16[2,512,512]{2,1,0:T(8,128)(2,1)S(1)}, bf16[2,512,512]{2,1,0:T(8,128)(2,1)}, u32[]{:S(2)}) copy-start(bf16[2,512,512]{2,1,0:T(8,128)(2,1)} %param.24) | copy-start | bytes 3145732
  150.8 4.0 %copy-start = (f32[2560,512]{0,1:T(8,128)S(1)}, f32[2560,512]{0,1:T(8,128)}, u32[]{:S(2)}) copy-start(f32[2560,512]{0,1:T(8,128)} %get-tuple-element.27) | copy-start | bytes 15728644
  161.0 5.9 %copy-start.5 = (f32[320,512]{1,0:T(8,128)S(1)}, f32[320,512]{1,0:T(8,128)}, u32[]{:S(2)}) copy-start(f32[320,512]{1,0:T(8,128)} %convolution_add_fusion.1) | copy-start | bytes 1966084
  166.9 4.1 %copy-start.4 = (bf16[2,512,512]{2,1,0:T(8,128)(2,1)S(1)}, bf16[2,512,512]{2,1,0:T(8,128)(2,1)}, u32[]{:S(2)}) copy-start(bf16[2,512,512]{2,1,0:T(8,128)(2,1)} %param.29) | copy-start | bytes 3145732
where the time goes:
time: 174 us; the launch traced here: 173 us
  matrix products  64.8 us (37%)
  local copies, waits for them, and re-layouts  45.2 us (26%)
  other arithmetic  24.3 us (14%)
  starting transfers between devices  20.1 us (12%)
  waiting for transfers between devices  17.6 us (10%)
    dot_general x8, matrix products, perceptron(): jnp.dot(pieces[position], first_weight[position * columns:(position + 1)...  35.6 us
    dot_general x4, matrix products, perceptron(): result = jnp.dot(active, second_weight, preferred_element_type=jnp.float32)  23 us
    all_to_all x2, waiting for transfers between devices, fetch_halo(): lax.all_to_all(outgoing, ('patch', 'band'), split_axis=0, concat_axis=0,...  17.6 us
    all_to_all x2, starting transfers between devices, fetch_halo(): lax.all_to_all(outgoing, ('patch', 'band'), split_axis=0, concat_axis=0,...  16.6 us
    gather x2, local copies, waits for them, and re-layouts, shards(): sender_table[edge_sender]  16.4 us
    unnamed x32, local copies, waits for them, and re-layouts  14.5 us
    add x2, other arithmetic, shards(): edge_state + jnp.where(usable[:, None], update, jnp.zeros_like(update))  12.5 us
    gather x2, local copies, waits for them, and re-layouts, fetch_halo(): outgoing = node_low[send_lists]  10.2 us
  transfers between devices with their start and end apart: 3, of which 2 were waited for; matrix products, arithmetic and copies ran while one was open for 19% of the time, Pallas kernels for 0%

commit v1 on v0

--- a/solution.py
+++ b/solution.py
@@ -56,7 +56,9 @@
         -1
     )
     first_rows = None
-    node_state = lax.all_to_all(latents, "band", split_axis=0, concat_axis=1, tiled=True)
+    parts = jnp.split(latents, lax.axis_size("band"), axis=0)
+    received = lax.all_to_all(jnp.stack(parts), "band", 0, 0)
+    node_state = jnp.concatenate(received, axis=1)
     edge_state = edge_latents
     node_count = node_state.shape[0]
     matches = jnp.arange(node_count, dtype=jnp.int32)[:, None] == edge_receiver[None, :]

time: 174 us -> 176 us (1.011)
  no operation moved by 1% of the time
where the time goes in v1:
time: 176 us; the launch traced here: 175 us
  matrix products  64.8 us (37%)
  local copies, waits for them, and re-layouts  46.4 us (26%)
  other arithmetic  25.2 us (14%)
  starting transfers between devices  20.1 us (11%)
  waiting for transfers between devices  17.6 us (10%)
    dot_general x8, matrix products, perceptron(): jnp.dot(pieces[position], first_weight[position * columns:(position + 1)...  35.6 us
    dot_general x4, matrix products, perceptron(): result = jnp.dot(active, second_weight, preferred_element_type=jnp.float32)  23.1 us
    all_to_all x2, waiting for transfers between devices, fetch_halo(): lax.all_to_all(outgoing, ('patch', 'band'), split_axis=0, concat_axis=0,...  17.6 us
    all_to_all x2, starting transfers between devices, fetch_halo(): lax.all_to_all(outgoing, ('patch', 'band'), split_axis=0, concat_axis=0,...  16.6 us
    gather x2, local copies, waits for them, and re-layouts, shards(): sender_table[edge_sender]  16.4 us
    unnamed x32, local copies, waits for them, and re-layouts  14.5 us
    add x2, other arithmetic, shards(): edge_state + jnp.where(usable[:, None], update, jnp.zeros_like(update))  12.5 us
    gather x2, local copies, waits for them, and re-layouts, fetch_halo(): outgoing = node_low[send_lists]  10.2 us
  transfers between devices with their start and end apart: 3, of which 2 were waited for; matrix products, arithmetic and copies ran while one was open for 19% of the time, Pallas kernels for 0%

profile of v1, /device:TPU:1, one launch (start us, length us, event | category | flops | bytes accessed | tf_op | source)
XLA Modules:
  0.0 174.9 jit_solution(10796314809711544578)
XLA Ops:
  0.6 1.1 slice_bitcast_fusion.1
  1.7 0.9 pad_maximum_fusion.2
  2.6 3.5 %all-to-all-start = ((f32[2,320,256]{2,1,0:T(8,128)}), f32[2,320,256]{2,1,0:T(8,128)S(1)}, u32[]{:S(2)}, u32[]{:S(2)}) async-start(f32[2,320,256]{2,1,0:T(8,128)} %pad_maximum_fusion.2), calls=%async_computation | async-start | bytes 1310720 | tf_op jit(solution)/shard_map/all_to_all | solution.py:60
  6.1 0.7 compare_select_fusion.1
  6.8 0.1 copy.23
  6.9 0.1 reshape.138
  7.1 0.8 fusion.90
  7.8 0.8 fusion.88
  8.6 0.8 fusion.89
  9.4 0.8 fusion.91
  10.1 0.8 fusion.86
  10.9 6.4 %fusion.6 = f32[2560,512]{1,0:T(8,128)} fusion(f32[2560,512]{1,0:T(8,128)} %param.17, bf16[2,1536,512]{2,1,0:T(8,128)(2,1)} %param.22), kind=kOutput, calls=%fused_computation.17 | convolution fusion | flops 1343488000 | bytes 11010048 | tf_op jit(solution)/shard_map/dot_general | solution.py:19
  17.3 0.0 copy-done.9
  17.3 0.1 fusion.82
  17.4 0.0 copy-done.7
  17.4 0.0 all-to-all-done
  17.4 0.1 copy.26
  17.6 5.1 %gather_fusion = bf16[1024,512]{1,0:T(8,128)(2,1)} fusion(bf16[320,512]{1,0:T(8,128)(2,1)S(1)} %convert_element_type.50, s32[1024]{0:T(1024)S(1)} %broadcast_clamp_fusion), kind=kCustom, calls=%fused_computation | custom fusion | bytes 2101248 | tf_op jit(solution)/shard_map/gather | solution.py:30
  22.6 12.5 %all-to-all-start.1 = ((bf16[128,8,512]{2,1,0:T(8,128)(2,1)}), bf16[128,8,512]{2,1,0:T(8,128)(2,1)}, u32[]{:S(2)}, u32[]{:S(2)}) async-start(bf16[128,8,512]{2,1,0:T(8,128)(2,1)} %bitcast.107), calls=%async_computation.1 | async-start | bytes 2097152 | tf_op jit(solution)/shard_map/all_to_all | solution.py:31
  35.2 0.0 copy-start.8
  35.2 0.0 copy-start.12
  35.2 5.9 %copy.24 = f32[2560,512]{0,1:T(8,128)} copy(f32[2560,512]{1,0:T(8,128)} %param.17) | data formatting | bytes 10485760 | tf_op args[1]
  41.1 0.0 copy-done.8
  41.2 2.2 %convolution_add_fusion.3 = f32[320,512]{1,0:T(8,128)} fusion(bf16[320,512]{1,0:T(8,128)(2,1)S(1)} %bitcast.109, bf16[2,1024,512]{2,1,0:T(8,128)(2,1)} %param.27, f32[512]{0:T(512)S(1)} %bitcast.117), kind=kOutput, calls=%fused_computation.35 | convolution fusion | flops 167936000 | bytes 1509376 | tf_op jit(solution)/shard_map/dot_general | solution.py:19
  43.4 0.0 copy-done.12
  43.4 3.0 %convolution_convert_fusion.1 = bf16[2560,512]{1,0:T(8,128)(2,1)} fusion(bf16[320,512]{1,0:T(8,128)(2,1)S(1)} %convert_element_type.50, s32[2560]{0:T(1024)S(1)} %copy-done.12), kind=kOutput, calls=%fused_computation.11 | convolution fusion | flops 840990720 | bytes 2959360 | tf_op jit(solution)/shard_map/dot_general | solution.py:71
  46.4 8.1 %all-to-all-done.1 = bf16[128,8,512]{2,1,0:T(8,128)(2,1)} async-done(((bf16[128,8,512]{2,1,0:T(8,128)(2,1)}), bf16[128,8,512]{2,1,0:T(8,128)(2,1)}, u32[]{:S(2)}, u32[]{:S(2)}) %all-to-all-start.1) | async-done | bytes 1048608 | tf_op jit(solution)/shard_map/all_to_all | solution.py:31
  54.5 1.3 pad_maximum_fusion
  55.9 8.2 %gather_fusion.1 = bf16[2560,512]{1,0:T(8,128)(2,1)} fusion(bf16[1344,512]{1,0:T(8,128)(2,1)S(1)} %pad_maximum_fusion, s32[3072]{0:T(1024)S(1)} %pad_clamp_fusion), kind=kCustom, calls=%fused_computation.1 | custom fusion | bytes 5253120 | tf_op jit(solution)/shard_map/gather | solution.py:76
  64.1 5.8 %fusion.61 = f32[2560,512]{1,0:T(8,128)} fusion(bf16[2560,512]{1,0:T(8,128)(2,1)} %gather_fusion.1, bf16[2,1536,512]{2,1,0:T(8,128)(2,1)} %param.22), kind=kOutput, calls=%fused_computation.60 | convolution fusion | flops 1342177280 | bytes 8388608 | tf_op jit(solution)/shard_map/dot_general | solution.py:19
  69.8 0.0 copy-done.10
  69.8 11.1 %fusion.92 = (f32[2560]{0:T(1024)S(1)}, f32[2560,512]{0,1:T(8,128)}) fusion(bf16[2,512,512]{2,1,0:T(8,128)(2,1)S(1)} %copy-done.10, f32[2560,512]{1,0:T(8,128)} %fusion.61, f32[2560,512]{1,0:T(8,128)} %fusion.6, bf16[2560,512]{1,0:T(8,128)(2,1)} %convolution_convert_fusion.1, f32[512]{0:T(512)S(1)} %bitcast.123, bf16[2,1536,512]{2,1,0:T(8,128)(2,1)} %param.22), kind=kOutput, calls=%fused_computation.104 | convolution fusion | flops 2696148480 | bytes 19410944 | tf_op jit(solution)/shard_map/dot_general | solution.py:25
  81.0 3.2 %multiply_reduce_fusion.1 = f32[2560]{0:T(1024)S(1)} fusion(f32[2560,512]{0,1:T(8,128)} %get-tuple-element.21, f32[2560]{0:T(1024)S(1)} %broadcast_multiply_fusion.1), kind=kLoop, calls=%fused_computation.8 | loop fusion | flops 3929600 | bytes 5263360 | tf_op jit(solution)/shard_map/reduce_sum | solution.py:11
  84.2 0.8 copy-done.1
  85.0 6.3 %select_add_fusion.1 = f32[2560,512]{0,1:T(8,128)} fusion(f32[2560,512]{0,1:T(8,128)} %copy.24, f32[2560,512]{0,1:T(8,128)S(1)} %copy-done.1, f32[512]{0:T(512)S(1)} %bitcast.121, f32[512]{0:T(512)S(1)} %bitcast.120, f32[2560]{0:T(1024)S(1)} %add_rsqrt_fusion.1, f32[2560]{0:T(1024)S(1)} %broadcast_multiply_fusion.1, pred[2560]{0:T(1024)(128)(4,1)S(1)} %fusion.82), kind=kLoop, calls=%fused_computation.7 | loop fusion | flops 7864320 | bytes 15755776 | tf_op jit(solution)/shard_map/add | solution.py:83
  91.3 0.0 copy-done.6
  91.3 4.1 %multiply_convert_fusion.3 = bf16[320,512]{1,0:T(8,128)(2,1)S(1)} fusion(f32[320,512]{1,0:T(8,128)S(1)} %copy-done.6, f32[2560,512]{0,1:T(8,128)} %select_add_fusion.1, s32[2560]{0:T(1024)S(1)} %copy-done.12, pred[2560]{0:T(1024)(128)(4,1)S(1)} %fusion.82, bf16[2,1024,512]{2,1,0:T(8,128)(2,1)} %param.27), kind=kOutput, calls=%fused_computation.45 | convolution fusion | flops 1010728960 | bytes 6763008 | tf_op jit(solution)/shard_map/dot_general | solution.py:19
  95.4 0.0 copy-done.3
  95.4 0.4 fusion.95
  95.8 0.2 multiply_reduce_fusion.3
  96.1 0.2 fusion.85
  96.3 5.1 %gather_fusion.2 = bf16[1024,512]{1,0:T(8,128)(2,1)} fusion(bf16[320,512]{1,0:T(8,128)(2,1)S(1)} %fusion.85, s32[1024]{0:T(1024)S(1)} %broadcast_clamp_fusion), kind=kCustom, calls=%fused_computation.2 | custom fusion | bytes 2101248 | tf_op jit(solution)/shard_map/gather | solution.py:30
  101.4 4.1 %all-to-all-start.2 = ((bf16[128,8,512]{2,1,0:T(8,128)(2,1)}), bf16[128,8,512]{2,1,0:T(8,128)(2,1)S(1)}, u32[]{:S(2)}, u32[]{:S(2)}) async-start(bf16[128,8,512]{2,1,0:T(8,128)(2,1)} %bitcast.24), calls=%async_computation.2 | async-start | bytes 2097152 | tf_op jit(solution)/shard_map/all_to_all | solution.py:31
  105.5 0.0 slice-start
  105.5 2.4 %convolution_add_fusion.1 = f32[320,512]{1,0:T(8,128)} fusion(bf16[320,512]{1,0:T(8,128)(2,1)S(1)} %fusion.85, bf16[2,1024,512]{2,1,0:T(8,128)(2,1)} %param.27, f32[512]{0:T(512)S(1)} %bitcast.116), kind=kOutput, calls=%fused_computation.33 | convolution fusion | flops 167936000 | bytes 1509376 | tf_op jit(solution)/shard_map/dot_general | solution.py:19
  107.9 3.0 %convolution_convert_fusion = bf16[2560,512]{1,0:T(8,128)(2,1)} fusion(bf16[320,512]{1,0:T(8,128)(2,1)S(1)} %fusion.85, s32[2560]{0:T(1024)S(1)} %copy-done.12), kind=kOutput, calls=%fused_computation.10 | convolution fusion | flops 840990720 | bytes 2959360 | tf_op jit(solution)/shard_map/dot_general | solution.py:71
  110.9 0.0 slice-done
  110.9 0.0 slice-done.1
  110.9 4.9 %fusion.16 = f32[2560,512]{1,0:T(8,128)} fusion(f32[2560,512]{0,1:T(8,128)S(1)} %bitcast.102, bf16[2,1536,512]{2,1,0:T(8,128)(2,1)} %param.22), kind=kOutput, calls=%fused_computation.29 | convolution fusion | flops 1343488000 | bytes 11010048 | tf_op jit(solution)/shard_map/dot_general | solution.py:19
  115.9 9.5 %all-to-all-done.2 = bf16[128,8,512]{2,1,0:T(8,128)(2,1)S(1)} async-done(((bf16[128,8,512]{2,1,0:T(8,128)(2,1)}), bf16[128,8,512]{2,1,0:T(8,128)(2,1)S(1)}, u32[]{:S(2)}, u32[]{:S(2)}) %all-to-all-start.2) | async-done | bytes 1048608 | tf_op jit(solution)/shard_map/all_to_all | solution.py:31
  125.4 1.0 copy-done.2
  126.4 1.3 pad_maximum_fusion.1
  127.7 8.2 %gather_fusion.3 = bf16[2560,512]{1,0:T(8,128)(2,1)} fusion(bf16[1344,512]{1,0:T(8,128)(2,1)S(1)} %pad_maximum_fusion.1, s32[3072]{0:T(1024)S(1)} %pad_clamp_fusion), kind=kCustom, calls=%fused_computation.3 | custom fusion | bytes 5253120 | tf_op jit(solution)/shard_map/gather | solution.py:76
  135.9 5.8 %fusion.51 = f32[2560,512]{1,0:T(8,128)} fusion(bf16[2560,512]{1,0:T(8,128)(2,1)} %gather_fusion.3, bf16[2,1536,512]{2,1,0:T(8,128)(2,1)} %param.22), kind=kOutput, calls=%fused_computation.51 | convolution fusion | flops 1342177280 | bytes 8388608 | tf_op jit(solution)/shard_map/dot_general | solution.py:19
  141.7 0.0 copy-done.11
  141.7 11.1 %fusion.96 = (f32[2560]{0:T(1024)S(1)}, f32[2560,512]{0,1:T(8,128)}) fusion(bf16[2,512,512]{2,1,0:T(8,128)(2,1)S(1)} %copy-done.11, f32[2560,512]{1,0:T(8,128)} %fusion.51, f32[2560,512]{1,0:T(8,128)} %fusion.16, bf16[2560,512]{1,0:T(8,128)(2,1)} %convolution_convert_fusion, f32[512]{0:T(512)S(1)} %bitcast.122, bf16[2,1536,512]{2,1,0:T(8,128)(2,1)} %param.22), kind=kOutput, calls=%fused_computation.106 | convolution fusion | flops 2696148480 | bytes 19410944 | tf_op jit(solution)/shard_map/dot_general | solution.py:25
  152.8 3.2 %multiply_reduce_fusion = f32[2560]{0:T(1024)S(1)} fusion(f32[2560,512]{0,1:T(8,128)} %get-tuple-element.25, f32[2560]{0:T(1024)S(1)} %broadcast_multiply_fusion), kind=kLoop, calls=%fused_computation.5 | loop fusion | flops 3929600 | bytes 5263360 | tf_op jit(solution)/shard_map/reduce_sum | solution.py:11
  156.1 0.8 copy-done
  156.8 6.2 %select_add_fusion = f32[2560,512]{0,1:T(8,128)} fusion(f32[2560,512]{0,1:T(8,128)} %select_add_fusion.1, f32[2560,512]{0,1:T(8,128)S(1)} %copy-done, f32[512]{0:T(512)S(1)} %bitcast.119, f32[512]{0:T(512)S(1)} %bitcast.118, f32[2560]{0:T(1024)S(1)} %add_rsqrt_fusion, f32[2560]{0:T(1024)S(1)} %broadcast_multiply_fusion, pred[2560]{0:T(1024)(128)(4,1)S(1)} %fusion.82), kind=kLoop, calls=%fused_computation.4 | loop fusion | flops 7864320 | bytes 15755776 | tf_op jit(solution)/shard_map/add | solution.py:83
  163.0 5.9 %copy.25 = f32[2560,512]{1,0:T(8,128)} copy(f32[2560,512]{0,1:T(8,128)} %select_add_fusion) | data formatting | bytes 10485760
  169.0 4.1 %multiply_convert_fusion.2 = bf16[320,512]{1,0:T(8,128)(2,1)S(1)} fusion(f32[320,512]{1,0:T(8,128)S(1)} %copy-done.5, f32[2560,512]{0,1:T(8,128)} %select_add_fusion, s32[2560]{0:T(1024)S(1)} %copy-done.12, pred[2560]{0:T(1024)(128)(4,1)S(1)} %fusion.82, bf16[2,1024,512]{2,1,0:T(8,128)(2,1)} %param.27), kind=kOutput, calls=%fused_computation.42 | convolution fusion | flops 1010728960 | bytes 6763008 | tf_op jit(solution)/shard_map/dot_general | solution.py:19
  173.1 0.4 fusion.99
  173.5 0.2 multiply_reduce_fusion.2
  173.8 1.1 add_add_fusion
  (30 shorter events, 0.2 us)
Async XLA Ops:
  2.6 14.8 %all-to-all-start = ((f32[2,320,256]{2,1,0:T(8,128)}), f32[2,320,256]{2,1,0:T(8,128)S(1)}, u32[]{:S(2)}, u32[]{:S(2)}) async-start(f32[2,320,256]{2,1,0:T(8,128)} %pad_maximum_fusion.2), calls=%async_computation | async-start | bytes 1310720 | tf_op jit(solution)/shard_map/all_to_all | solution.py:60
  10.9 6.4 %copy-start.9 = (s32[20]{0:T(128)S(1)}, s32[20]{0:T(128)}, u32[]{:S(2)}) copy-start(s32[20]{0:T(128)} %param.20) | copy-start | bytes 244
  10.9 6.5 %copy-start.7 = (s32[2560]{0:T(1024)S(1)}, s32[2560]{0:T(1024)}, u32[]{:S(2)}) copy-start(s32[2560]{0:T(1024)} %param.18) | copy-start | bytes 30724
  22.6 31.9 %all-to-all-start.1 = ((bf16[128,8,512]{2,1,0:T(8,128)(2,1)}), bf16[128,8,512]{2,1,0:T(8,128)(2,1)}, u32[]{:S(2)}, u32[]{:S(2)}) async-start(bf16[128,8,512]{2,1,0:T(8,128)(2,1)} %bitcast.107), calls=%async_computation.1 | async-start | bytes 2097152 | tf_op jit(solution)/shard_map/all_to_all | solution.py:31
  35.2 5.9 %copy-start.8 = (f32[2,512]{1,0:T(2,128)S(1)}, f32[2,512]{1,0:T(2,128)}, u32[]{:S(2)}) copy-start(f32[2,512]{1,0:T(2,128)} %param.31) | copy-start | bytes 12292
  35.2 8.2 %copy-start.12 = (s32[2560]{0:T(1024)S(1)}, s32[2560]{0:T(1024)}, u32[]{:S(2)}) copy-start(s32[2560]{0:T(1024)} %param.19) | copy-start | bytes 30724
  64.1 5.8 %copy-start.10 = (bf16[2,512,512]{2,1,0:T(8,128)(2,1)S(1)}, bf16[2,512,512]{2,1,0:T(8,128)(2,1)}, u32[]{:S(2)}) copy-start(bf16[2,512,512]{2,1,0:T(8,128)(2,1)} %param.24) | copy-start | bytes 3145732
  81.0 4.0 %copy-start.1 = (f32[2560,512]{0,1:T(8,128)S(1)}, f32[2560,512]{0,1:T(8,128)}, u32[]{:S(2)}) copy-start(f32[2560,512]{0,1:T(8,128)} %get-tuple-element.21) | copy-start | bytes 15728644
  85.0 6.3 %copy-start.6 = (f32[320,512]{1,0:T(8,128)S(1)}, f32[320,512]{1,0:T(8,128)}, u32[]{:S(2)}) copy-start(f32[320,512]{1,0:T(8,128)} %convolution_add_fusion.3) | copy-start | bytes 1966084
  91.3 4.1 %copy-start.3 = (bf16[2,512,512]{2,1,0:T(8,128)(2,1)S(1)}, bf16[2,512,512]{2,1,0:T(8,128)(2,1)}, u32[]{:S(2)}) copy-start(bf16[2,512,512]{2,1,0:T(8,128)(2,1)} %param.29) | copy-start | bytes 3145732
  101.4 24.0 %all-to-all-start.2 = ((bf16[128,8,512]{2,1,0:T(8,128)(2,1)}), bf16[128,8,512]{2,1,0:T(8,128)(2,1)S(1)}, u32[]{:S(2)}, u32[]{:S(2)}) async-start(bf16[128,8,512]{2,1,0:T(8,128)(2,1)} %bitcast.24), calls=%async_computation.2 | async-start | bytes 2097152 | tf_op jit(solution)/shard_map/all_to_all | solution.py:31
  105.5 5.4 %slice-start = ((s8[5242880]{0:T(1024)(128)(4,1)}), s8[4194304]{0:T(1024)(128)(4,1)S(1)}, s32[]{:S(2)}) async-start(s8[5242880]{0:T(1024)(128)(4,1)} %bitcast.101), calls=%async_computation.3 | async-start | bytes 8388608
  107.9 3.1 %slice-start.1 = ((s8[5242880]{0:T(1024)(128)(4,1)}), s8[1048576]{0:T(1024)(128)(4,1)S(1)}, s32[]{:S(2)}) async-start(s8[5242880]{0:T(1024)(128)(4,1)} %bitcast.101), calls=%async_computation.4 | async-start | bytes 2097152
  125.4 1.0 copy-start.2
  135.9 5.8 %copy-start.11 = (bf16[2,512,512]{2,1,0:T(8,128)(2,1)S(1)}, bf16[2,512,512]{2,1,0:T(8,128)(2,1)}, u32[]{:S(2)}) copy-start(bf16[2,512,512]{2,1,0:T(8,128)(2,1)} %param.24) | copy-start | bytes 3145732
  152.8 4.0 %copy-start = (f32[2560,512]{0,1:T(8,128)S(1)}, f32[2560,512]{0,1:T(8,128)}, u32[]{:S(2)}) copy-start(f32[2560,512]{0,1:T(8,128)} %get-tuple-element.25) | copy-start | bytes 15728644
  163.0 5.9 %copy-start.5 = (f32[320,512]{1,0:T(8,128)S(1)}, f32[320,512]{1,0:T(8,128)}, u32[]{:S(2)}) copy-start(f32[320,512]{1,0:T(8,128)} %convolution_add_fusion.1) | copy-start | bytes 1966084
  169.0 4.1 %copy-start.4 = (bf16[2,512,512]{2,1,0:T(8,128)(2,1)S(1)}, bf16[2,512,512]{2,1,0:T(8,128)(2,1)}, u32[]{:S(2)}) copy-start(bf16[2,512,512]{2,1,0:T(8,128)(2,1)} %param.29) | copy-start | bytes 3145732
